TPU v7x, 8 devices: a whole 2x2x1 slice. The times are simulated.
8 devices in a mesh: dp: 1 (over z), vp: 8 (over y, x, core).
Axes of the slice: x: 2, y: 2, z: 1, core: 2. Of those that a mesh axis runs over, the one named last changes fastest.
Arguments:
- hidden: bfloat16 [2048, 2048], P(('dp', 'vp'))
- labels: int32 [2048], P(('dp', 'vp'))
- loss_weight: float32 [2048], P(('dp', 'vp'))
- norm_gain: float32 [2048], replicated
- w_unembed: bfloat16 [2048, 32128], P(None, 'vp')
Outputs:
- output 1: float32 [1], P('dp')
- output 2: bfloat16 [2048, 2048], P(('dp', 'vp'))
- output 3: float32 [2048, 32128], P('dp', 'vp')
- output 4: float32 [2048], P('dp')
All inputs are finite; a program needn't handle non-finite values.
Results may differ from a plain program's by a relative error of at most 0.001.
Values are sent between devices in bfloat16 or wider.
A program may use at most 1 GiB of HBM per device.

v0:
```python
import jax
import jax.numpy as jnp
from jax import lax
from jax.sharding import PartitionSpec as P

NORM_EPS = 1e-5
PAD_COLS = 128


def solution(mesh):
    group_size = mesh.shape["vp"]

    def local_step(hidden, labels, loss_weight, norm_gain, w_local):
        vocab_local = w_local.shape[1]
        vocab_real = vocab_local * group_size - PAD_COLS
        x_float = hidden.astype(jnp.float32)
        inv_rms = lax.rsqrt(jnp.mean(x_float * x_float, axis=-1, keepdims=True) + NORM_EPS)
        x_norm = x_float * inv_rms
        normed = (x_norm * norm_gain).astype(jnp.bfloat16)
        normed_all = lax.all_gather(normed, "vp", axis=0, tiled=True)
        labels_all = lax.all_gather(labels, "vp", axis=0, tiled=True)
        weights_all = lax.all_gather(loss_weight, "vp", axis=0, tiled=True)
        col_ids = lax.axis_index("vp") * vocab_local + lax.broadcasted_iota(jnp.int32, (1, vocab_local), 1)
        logits = jnp.dot(normed_all, w_local, preferred_element_type=jnp.float32)
        logits = jnp.where(col_ids < vocab_real, logits, -jnp.inf)
        is_target = col_ids == labels_all[:, None]
        row_max = lax.pmax(jnp.max(logits, axis=1), "vp")
        shifted = jnp.exp(logits - row_max[:, None])
        sum_exp = lax.psum(jnp.sum(shifted, axis=1), "vp")
        target = lax.psum(jnp.sum(jnp.where(is_target, logits, 0.0), axis=1), "vp")
        log_norm = row_max + jnp.log(sum_exp)
        tok_scale = weights_all / jnp.sum(weights_all)
        mean_loss = jnp.sum(tok_scale * (log_norm - target)).reshape(1)
        prob_all = shifted / sum_exp[:, None]
        d_logits = ((prob_all - jnp.where(is_target, 1.0, 0.0)) * tok_scale[:, None]).astype(jnp.bfloat16)
        d_unembed = lax.dot_general(normed_all, d_logits, (((0,), (0,)), ((), ())), preferred_element_type=jnp.float32)
        d_part = lax.dot_general(d_logits, w_local, (((1,), (1,)), ((), ())), preferred_element_type=jnp.float32)
        d_normed = lax.psum_scatter(d_part, "vp", scatter_dimension=0, tiled=True)
        grad_hat = d_normed * norm_gain
        d_input = inv_rms * (grad_hat - x_norm * jnp.mean(grad_hat * x_norm, axis=-1, keepdims=True))
        d_norm_gain = lax.psum(jnp.sum(d_normed * x_norm, axis=0), "vp")
        return mean_loss, d_input.astype(jnp.bfloat16), d_unembed, d_norm_gain

    return jax.shard_map(
        local_step,
        mesh=mesh,
        in_specs=(P(("dp", "vp"), None), P(("dp", "vp")), P(("dp", "vp")), P(None), P(None, "vp")),
        out_specs=(P("dp"), P(("dp", "vp"), None), P("dp", "vp"), P("dp")),
        check_vma=False,
    )
```

profile of v0, /device:TPU:0, one launch (start us, length us, event | category | flops | bytes accessed | tf_op | source)
XLA Modules:
  0.0 377.8 jit_solution(14138713478788201035)
XLA Ops:
  7.2 0.0 all-gather.4.cloned.1.call-start
  7.2 1.5 fusion.15
  8.7 0.0 copy-start.9
  8.7 0.6 copy-done.9
  9.3 2.5 fusion.9
  11.8 0.0 all-gather.4.cloned.1.call-update
  11.9 0.0 reduce-scatter.2.cloned.1.call-start
  11.9 13.7 %all-gather = f32[8,1,256]{2,1,0:T(1,128)S(1)} all-gather(f32[1,1,256]{2,1,0:T(1,128)} %bitcast.18), channel_id=1, replica_groups=mesh['dp'=1,'vp'=8] {'vp'}, dimensions={0}, use_global_device_ids=true | all-gather | bytes 9216 | tf_op jit(solution)/shard_map/all_gather | solution.py:22
  25.6 0.6 reduce_sum.63
  26.2 10.8 %all-gather.1 = s32[8,1,256]{2,1,0:T(1,128)S(1)} all-gather(s32[1,1,256]{2,1,0:T(1,128)} %bitcast.19), channel_id=1, replica_groups=mesh['dp'=1,'vp'=8] {'vp'}, dimensions={0}, use_global_device_ids=true | all-gather | bytes 9216 | tf_op jit(solution)/shard_map/all_gather | solution.py:21
  37.0 0.7 broadcast_divide_fusion
  37.7 0.0 copy-start.4
  37.7 25.7 %all-gather.4.cloned.1.call-done = bf16[2048,2048]{1,0:T(8,128)(2,1)} async-done(((bf16[256,2048]{1,0:T(8,128)(2,1)}), bf16[2048,2048]{1,0:T(8,128)(2,1)}) %all-gather.4.cloned.1.call-update) | async-done | bytes 8388624 | tf_op jit(solution)/shard_map/all_gather | solution.py:20
  63.3 42.8 %select_reduce_fusion = (f32[2048]{0:T(1024)S(1)}, f32[2048,4016]{0,1:T(8,128)}) fusion(pred[4016]{0:T(1024)(128)(4,1)S(1)} %broadcast_compare_fusion, bf16[2048,2048]{1,0:T(8,128)(2,1)} %all-gather.4.cloned.1.call-done, bf16[2048,4016]{0,1:T(8,128)(2,1)} %param.9), kind=kOutput, calls=%fused_computation.8 | convolution fusion | flops 33705097216 | bytes 57749424 | tf_op jit(solution)/shard_map/dot_general | solution.py:24
  106.2 22.2 %pmax.7 = f32[2048]{0:T(1024)S(1)} all-reduce(f32[2048]{0:T(1024)S(1)} %get-tuple-element.10), channel_id=1, replica_groups=mesh['dp'=1,'vp'=8] {'vp'}, use_global_device_ids=true, to_apply=%region_3.4 | all-reduce | flops 2048 | bytes 16384 | tf_op jit(solution)/shard_map/pmax | solution.py:27
  128.4 0.0 copy-start.1
  128.4 16.5 %fusion.4 = (f32[2048]{0:T(1024)S(1)}, f32[2048]{0:T(1024)}) fusion(f32[2048,4016]{0,1:T(8,128)} %get-tuple-element.11, f32[2048]{0:T(1024)S(1)} %pmax.7, pred[4016]{0:T(1024)(128)(4,1)S(1)} %broadcast_compare_fusion, s32[2048]{0:T(1024)S(1)} %bitcast.14, s32[4016]{0:T(1024)S(1)} %iota_add_fusion), kind=kLoop, calls=%fused_computation.7 | loop fusion | flops 49344512 | bytes 32951920 | tf_op jit(solution)/shard_map/reduce_sum | solution.py:29
  144.9 24.2 %psum.21 = f32[2048]{0:T(1024)S(1)} all-reduce(f32[2048]{0:T(1024)S(1)} %get-tuple-element.4), channel_id=1, replica_groups=mesh['dp'=1,'vp'=8] {'vp'}, use_global_device_ids=true, to_apply=%region_5.6 | all-reduce | flops 2048 | bytes 16384 | tf_op jit(solution)/shard_map/psum | solution.py:29
  169.1 0.0 copy-start.6
  169.1 0.0 copy-done.4
  169.1 0.0 copy-done.1
  169.1 22.1 %fusion.3 = bf16[2048,4016]{0,1:T(8,128)(2,1)} fusion(f32[2048,4016]{0,1:T(8,128)} %get-tuple-element.11, f32[2048]{0:T(1024)S(1)} %bitcast.16, f32[2048]{0:T(1024)S(1)} %psum.21, s32[2048]{0:T(1024)S(1)} %bitcast.15, f32[2048]{0:T(1024)S(1)} %pmax.7, s32[4016]{0:T(1024)S(1)} %iota_add_fusion, pred[4016]{0:T(1024)(128)(4,1)S(1)} %broadcast_compare_fusion), kind=kLoop, calls=%fused_computation.5 | loop fusion | flops 65798144 | bytes 49401456 | tf_op jit(solution)/shard_map/convert_element_type | solution.py:35
  191.2 0.0 copy-done.6
  191.2 43.4 %fusion.16 = f32[2048,2048]{1,0:T(8,128)} fusion(bf16[2048,4016]{0,1:T(8,128)(2,1)} %fusion.3, bf16[2048,4016]{0,1:T(8,128)(2,1)} %param.9), kind=kOutput, calls=%fused_computation.28 | convolution fusion | flops 33688649728 | bytes 49676288 | tf_op jit(solution)/shard_map/dot_general | solution.py:37
  234.6 0.0 reduce-scatter.2.cloned.1.call-update
  234.6 0.0 copy-start
  234.6 0.0 copy-start.3
  234.6 0.0 copy-start.10
  234.6 0.0 copy-start.8
  234.7 0.0 copy-start.2
  234.7 0.0 copy-start.5
  234.7 0.0 copy-start.7
  234.7 42.5 %fusion.17 = f32[2048,4016]{0,1:T(8,128)} fusion(bf16[2048,4016]{0,1:T(8,128)(2,1)} %fusion.3, bf16[2048,2048]{1,0:T(8,128)(2,1)} %all-gather.4.cloned.1.call-done), kind=kOutput, calls=%fused_computation.29 | convolution fusion | flops 33688649728 | bytes 57737216 | tf_op jit(solution)/shard_map/dot_general | solution.py:36
  277.1 65.4 %reduce-scatter.2.cloned.1.call-done = f32[256,2048]{1,0:T(8,128)} async-done(((f32[2048,2048]{1,0:T(8,128)}), f32[256,2048]{1,0:T(8,128)}) %reduce-scatter.2.cloned.1.call-update) | async-done | bytes 2097168 | tf_op jit(solution)/shard_map/reduce_scatter | solution.py:38
  342.6 0.0 copy-done
  342.6 0.0 copy-done.3
  342.6 0.0 copy-done.10
  342.6 2.2 fusion.14
  344.8 0.0 copy-done.8
  344.8 22.4 %all-reduce = (f32[2048]{0:T(1024)S(1)}, f32[2048]{0:T(1024)}) all-reduce(f32[2048]{0:T(1024)S(1)} %copy-done.8, f32[2048]{0:T(1024)S(1)} %get-tuple-element.6), channel_id=1, replica_groups=mesh['dp'=1,'vp'=8] {'vp'}, use_global_device_ids=true, to_apply=%region_7.8 | all-reduce | flops 4096 | bytes 32768 | tf_op jit(solution)/shard_map/psum | solution.py:30
  367.2 0.0 copy-done.2
  367.2 0.0 copy-done.5
  367.2 0.0 copy-done.7
  367.2 0.6 multiply_reduce_fusion
  367.9 3.1 fusion.13
  (4 shorter events, 0.0 us)
Async XLA Ops:
  7.2 56.2 %all-gather.4.cloned.1.call-start = ((), (), s32[]{:S(2)}) async-start(), calls=%async_computation.1 | async-start | bytes 9437184 | tf_op jit(solution)/shard_map/all_gather | solution.py:20
  8.7 0.6 copy-start.9
  11.9 330.7 %reduce-scatter.2.cloned.1.call-start = ((), (), s32[]{:S(2)}) async-start(), calls=%async_computation.2 | async-start | bytes 18874368 | tf_op jit(solution)/shard_map/reduce_scatter | solution.py:38
  37.7 131.4 %copy-start.4 = (f32[1,8,256]{2,1,0:T(8,128)}, f32[1,8,256]{2,1,0:T(8,128)S(1)}, u32[]{:S(2)}) copy-start(f32[1,8,256]{2,1,0:T(8,128)S(1)} %broadcast_divide_fusion) | copy-start | bytes 24580
  128.4 40.7 %copy-start.1 = (f32[2048]{0:T(1024)}, f32[2048]{0:T(1024)S(1)}, u32[]{:S(2)}) copy-start(f32[2048]{0:T(1024)S(1)} %pmax.7) | copy-start | bytes 24580
  169.1 22.1 %copy-start.6 = (f32[2048]{0:T(1024)}, f32[2048]{0:T(1024)S(1)}, u32[]{:S(2)}) copy-start(f32[2048]{0:T(1024)S(1)} %psum.21) | copy-start | bytes 24580
  234.6 107.9 %copy-start = (bf16[256,2048]{1,0:T(8,128)(2,1)S(1)}, bf16[256,2048]{1,0:T(8,128)(2,1)}, u32[]{:S(2)}) copy-start(bf16[256,2048]{1,0:T(8,128)(2,1)} %param.5) | copy-start | bytes 3145732
  234.6 107.9 %copy-start.3 = (f32[2048]{0:T(1024)S(1)}, f32[2048]{0:T(1024)}, u32[]{:S(2)}) copy-start(f32[2048]{0:T(1024)} %param.8) | copy-start | bytes 24580
  234.6 107.9 %copy-start.10 = (f32[256]{0:T(256)S(1)}, f32[256]{0:T(256)}, u32[]{:S(2)}) copy-start(f32[256]{0:T(256)} %copy-done.9) | copy-start | bytes 3076
  234.6 110.2 %copy-start.8 = (f32[2048]{0:T(1024)S(1)}, f32[2048]{0:T(1024)}, u32[]{:S(2)}) copy-start(f32[2048]{0:T(1024)} %get-tuple-element.5) | copy-start | bytes 24580
  234.7 132.6 %copy-start.2 = (f32[2048]{0:T(1024)S(1)}, f32[2048]{0:T(1024)}, u32[]{:S(2)}) copy-start(f32[2048]{0:T(1024)} %copy-done.1) | copy-start | bytes 24580
  234.7 132.6 %copy-start.5 = (f32[1,8,256]{2,1,0:T(8,128)S(1)}, f32[1,8,256]{2,1,0:T(8,128)}, u32[]{:S(2)}) copy-start(f32[1,8,256]{2,1,0:T(8,128)} %copy-done.4) | copy-start | bytes 24580
  234.7 132.5 %copy-start.7 = (f32[2048]{0:T(1024)S(1)}, f32[2048]{0:T(1024)}, u32[]{:S(2)}) copy-start(f32[2048]{0:T(1024)} %copy-done.6) | copy-start | bytes 24580
Sparse Core Ops, SparseCore 0:
  12.0 51.3 all-gather.3
  234.7 107.7 reduce-scatter.1
where the time goes:
time: 379 us; the launch traced here: 378 us
  matrix products  129 us (34%)
  blocking collectives  93.3 us (25%)
  waiting for transfers between devices  91.1 us (24%)
  other arithmetic  49.8 us (13%)
  between operations  14.2 us (4%)
    reduce_scatter x1, waiting for transfers between devices, local_step(): d_normed = lax.psum_scatter(d_part, 'vp', scatter_dimension=0, tiled=True)  65.4 us
    dot_general x1, matrix products, local_step(): lax.dot_general(d_logits, w_local, (((1,), (1,)), ((), ())), preferred_el...  43.4 us
    dot_general x1, matrix products, local_step(): logits = jnp.dot(normed_all, w_local, preferred_element_type=jnp.float32)  42.8 us
    dot_general x1, matrix products, local_step(): lax.dot_general(normed_all, d_logits, (((0,), (0,)), ((), ())), preferred...  42.5 us
    all_gather x1, waiting for transfers between devices, local_step(): normed_all = lax.all_gather(normed, 'vp', axis=0, tiled=True)  25.7 us
    psum x1, blocking collectives, local_step(): sum_exp = lax.psum(jnp.sum(shifted, axis=1), 'vp')  24.2 us
    psum x1, blocking collectives, local_step(): target = lax.psum(jnp.sum(jnp.where(is_target, logits, 0.0), axis=1), 'vp')  22.4 us
    pmax x1, blocking collectives, local_step(): row_max = lax.pmax(jnp.max(logits, axis=1), 'vp')  22.2 us
  transfers between devices with their start and end apart: 2, of which 2 were waited for; matrix products, arithmetic and copies ran while one was open for 12% of the time, Pallas kernels for 0%

commit v1 on v0

v1 whole, which is shorter than its diff:
```python
import functools

import jax
import jax.numpy as jnp
from jax import lax
from jax.experimental import pallas as pl
from jax.experimental.pallas import tpu as pltpu
from jax.sharding import PartitionSpec as P

NORM_EPS = 1e-5
PAD_COLS = 128
LANES = 128
VT = 1024
NT = 1024
LOWEST = -3.0e38
MESH = pl.DeviceIdType.MESH
VMEM_BYTES = 67_000_000


def xor_peers(me):
    step_core = 1 - 2 * (me % 2)
    step_x = 2 - 4 * ((me // 2) % 2)
    step_y = 4 - 8 * (me // 4)
    return [me + (r % 2) * step_core + ((r // 2) % 2) * step_x + (r // 4) * step_y for r in range(8)]


def unit_of(rel, half):
    if rel in (0, 1):
        return 2 * rel + half
    if rel in (6, 7):
        return 12 + 2 * (rel - 6) + half
    return {2: 4, 4: 5, 3: 6, 5: 7}[rel] + 4 * half


def head_kernel(
    hidden_hbm, meta_ref, gain_ref, w_hbm,
    a_out, dz_out, px_out, py_out, pown_out, z_hbm, loss_ref,
    w_v, a_v, z_v, dz_v, meta_v, row_v, m_v, s_v, t_v, st_v, out_v, prt_v, drecv_v, dsend_v, hold_v, stage_v,
    ag_send, ag_recv, meta_send, meta_recv, st_send, st_recv, prt_send, prt_recv, d_send, d_recv,
    in_sem, w_sem, z_sem, a_sem, dz_sem, stage_sem, fin_sem, credit,
):
    me = lax.axis_index("vp")
    peers = xor_peers(me)
    vocab_local, width = w_hbm.shape
    vocab_real = 8 * vocab_local - PAD_COLS
    padded = w_v.shape[0]
    n_vt = padded // VT
    tok_dev = hidden_hbm.shape[0]
    chunk = 2 * tok_dev
    half = tok_dev // 2
    mine = tok_dev

    def remote(src, dst, send, recv, rel):
        return pltpu.make_async_remote_copy(
            src_ref=src, dst_ref=dst, send_sem=send, recv_sem=recv,
            device_id={"vp": peers[rel]}, device_id_type=MESH,
        )

    hidden_v = dz_v.at[0, 0:tok_dev, 0:width]
    hidden_copy = pltpu.make_async_copy(hidden_hbm, hidden_v, in_sem)
    hidden_copy.start()
    barrier = pltpu.get_barrier_semaphore()
    for r in range(1, 8):
        pl.semaphore_signal(barrier, inc=1, device_id={"vp": peers[r]}, device_id_type=MESH)

    def w_copy(j):
        hi = min((j + 1) * VT, vocab_local)
        return pltpu.make_async_copy(w_hbm.at[j * VT:hi], w_v.at[j * VT:hi], w_sem.at[j])

    for j in range(n_vt):
        w_copy(j).start()
    meta_v[0] = meta_ref[...]

    hidden_copy.wait()
    for b in range(0, tok_dev, 32):
        x = dz_v[0, b:b + 32, 0:width].astype(jnp.float32)
        inv_rms = lax.rsqrt(jnp.mean(x * x, axis=-1, keepdims=True) + NORM_EPS)
        a_v[b:b + 32, :] = (x * inv_rms * gain_ref[...]).astype(jnp.bfloat16)
    w_v[vocab_local:padded, :] = jnp.zeros((padded - vocab_local, width), jnp.bfloat16)
    pl.semaphore_wait(barrier, 7)

    metas = [remote(meta_v.at[0], meta_v.at[r], meta_send.at[r - 1], meta_recv.at[r - 1], r) for r in range(1, 8)]
    for copy in metas:
        copy.start()

    def ag(idx, src, dst, count, rel):
        return remote(
            a_v.at[src:src + count], a_v.at[dst:dst + count], ag_send.at[idx], ag_recv.at[idx], rel
        )

    c1, c2, c3 = chunk, 2 * chunk, 3 * chunk
    own_p = ag(0, 0, mine, mine, 1)
    x_h0 = ag(1, 0, c1, half, 2)
    y_h0 = ag(2, 0, c1 + half, half, 4)
    m1_p = ag(3, c1, c1 + mine, mine, 1)
    x_h1 = ag(4, half, c2, half, 2)
    y_h1 = ag(5, half, c2 + half, half, 4)
    m2_p = ag(6, c2, c2 + mine, mine, 1)
    d_h0 = ag(7, c1 + half, c3, half, 2)
    d_h1 = ag(8, c2, c3 + half, half, 4)
    d_p = ag(9, c3, c3 + mine, mine, 1)
    for copy in (x_h0, y_h0, own_p, x_h1, y_h1):
        copy.start()

    for copy in metas:
        copy.wait_recv()
    for rel in range(8):
        for h in range(2):
            u = unit_of(rel, h)
            row_v[:, u * LANES:(u + 1) * LANES] = meta_v[rel, :, h * LANES:(h + 1) * LANES]

    base_f = (me * vocab_local).astype(jnp.float32)
    local = row_v[0:1, :] - base_f
    row_v[0:1, :] = jnp.where(local < float(vocab_local), local, -1.0)
    valid = jnp.minimum(vocab_local, vocab_real - me * vocab_local)

    def chunk_at(c):
        return pl.ds(pl.multiple_of(c * chunk, chunk), chunk)

    def row_at(row, c, lt):
        return row_v[row:row + 1, pl.ds(pl.multiple_of(c * chunk + lt * LANES, LANES), LANES)]

    def a_copy(c):
        return pltpu.make_async_copy(a_v.at[chunk_at(c)], a_out.at[chunk_at(c)], a_sem.at[c])

    def z_copy(t):
        return pltpu.make_async_copy(z_v.at[t % 4], z_hbm.at[t], z_sem.at[t % 4])

    group = 256
    sub_f = lax.broadcasted_iota(jnp.int32, (8, LANES), 0).astype(jnp.float32)
    step_f = 8.0 * lax.broadcasted_iota(jnp.int32, (group // 8, 8, LANES), 0).astype(jnp.float32)

    def stats_pass(c, j):
        first = j == 0
        for lt in range(chunk // LANES):
            cols = slice(lt * LANES, (lt + 1) * LANES)
            lab = row_at(0, c, lt) - (j * VT).astype(jnp.float32) - sub_f
            m = jnp.where(first, LOWEST, m_v[:, cols])
            s = jnp.where(first, 0.0, s_v[:, cols])
            t = jnp.where(first, 0.0, t_v[:, cols])
            for b in range(0, VT, group):
                z = z_v[j, b:b + group, cols].reshape(group // 8, 8, LANES)
                m_new = jnp.maximum(m, jnp.max(z, axis=0))
                s = s * jnp.exp(m - m_new) + jnp.sum(jnp.exp(z - m_new[None]), axis=0)
                t += jnp.sum(jnp.where((lab - float(b))[None] == step_f, z, 0.0), axis=0)
                m = m_new
            m_v[:, cols] = m
            s_v[:, cols] = s
            t_v[:, cols] = t

    def st_copy(c, r):
        at = (slice(None), chunk_at(c))
        return remote(st_v.at[(0, *at)], st_v.at[(r, *at)], st_send.at[c * 7 + r - 1], st_recv.at[c * 7 + r - 1], r)

    def send_stats(c):
        m = m_v[...]
        m_row = jnp.max(m, axis=0, keepdims=True)
        st_v[0, 0:1, chunk_at(c)] = m_row
        st_v[0, 1:2, chunk_at(c)] = jnp.sum(s_v[...] * jnp.exp(m - m_row), axis=0, keepdims=True)
        st_v[0, 2:3, chunk_at(c)] = jnp.sum(t_v[...], axis=0, keepdims=True)
        for r in range(1, 8):
            st_copy(c, r).start()

    st_v[0] = jnp.zeros(st_v.shape[1:], jnp.float32)

    def forward_step(t, carry):
        c, j = t // n_vt, t % n_vt
        prev = jnp.maximum(t - 1, 0)
        for jj in range(n_vt):
            @pl.when(t == jj)
            def _():
                w_copy(jj).wait()

        @pl.when(t == 0)
        def _():
            own_p.wait_recv()

        @pl.when(t == n_vt)
        def _():
            x_h0.wait_recv()
            y_h0.wait_recv()
            m1_p.start()
            d_h0.start()
            m1_p.wait_recv()

        @pl.when(t == 2 * n_vt)
        def _():
            x_h1.wait_recv()
            y_h1.wait_recv()
            m2_p.start()
            d_h1.start()
            m2_p.wait_recv()

        @pl.when(t == 3 * n_vt)
        def _():
            d_h0.wait_recv()
            d_h1.wait_recv()
            d_p.start()
            d_p.wait_recv()

        @pl.when(j == 0)
        def _():
            a_copy(c).start()

        @pl.when(t >= n_vt)
        def _():
            z_copy(t - n_vt).wait()

        words = pl.ds(pl.multiple_of(j * VT, VT), VT)
        z_v[j] = lax.dot_general(
            w_v[words, :], a_v[chunk_at(c), :], (((1,), (1,)), ((), ())), preferred_element_type=jnp.float32
        )
        stats_pass(prev // n_vt, prev % n_vt)

        @pl.when(j == n_vt - 1)
        def _():
            low = (vocab_local - PAD_COLS) // 8 * 8 - (n_vt - 1) * VT
            ids = (n_vt - 1) * VT + low + lax.broadcasted_iota(jnp.int32, (VT - low, chunk), 0)
            z_v[j, low:VT, :] = jnp.where(ids < valid, z_v[j, low:VT, :], -jnp.inf)

        @pl.when(t < 3 * n_vt)
        def _():
            z_copy(t).start()

        @pl.when((j == 0) & (t > 0))
        def _():
            send_stats(prev // n_vt)

        return carry

    lax.fori_loop(0, 4 * n_vt, forward_step, 0)
    stats_pass(jnp.int32(3), jnp.int32(n_vt - 1))
    send_stats(jnp.int32(3))

    for copy in (x_h0, y_h0, own_p, x_h1, y_h1, m1_p, m2_p, d_h0, d_h1, d_p):
        copy.wait_send()
    for c in range(4):
        a_copy(c).wait()

    w_row = row_v[1:2, :]
    row_v[3:4, :] = w_row / jnp.sum(w_row)
    for c in range(4):
        for r in range(1, 8):
            st_copy(c, r).wait_recv()
    loss = jnp.zeros((1, LANES), jnp.float32)
    for rel in range(8):
        for h in range(2):
            u = unit_of(rel, h)
            parts = []
            for r in range(8):
                v = unit_of(rel ^ r, h)
                parts.append([st_v[r, i:i + 1, v * LANES:(v + 1) * LANES] for i in range(3)])
            row_max = functools.reduce(jnp.maximum, [p[0] for p in parts])
            row_sum = sum(p[1] * jnp.exp(p[0] - row_max) for p in parts)
            target = sum(p[2] for p in parts)
            log_norm = row_max + jnp.log(row_sum)
            row_v[2:3, u * LANES:(u + 1) * LANES] = log_norm
            loss += row_v[3:4, u * LANES:(u + 1) * LANES] * (log_norm - target)
    loss_ref[...] = jnp.broadcast_to(jnp.sum(loss, axis=1, keepdims=True), loss_ref.shape)

    per_half = n_vt // 2
    half_words = per_half * VT
    word_f = lax.broadcasted_iota(jnp.int32, (LANES, LANES), 0).astype(jnp.float32)

    def dz_pass(c, j, q):
        out_at = (q % 2) * 2 + j
        for lt in range(chunk // LANES):
            cols = slice(lt * LANES, (lt + 1) * LANES)
            log_norm, scale = row_at(2, c, lt), row_at(3, c, lt)
            lab = row_at(0, c, lt) - (j * half_words).astype(jnp.float32) - word_f
            to_a = pl.ds(pl.multiple_of(out_at * chunk + lt * LANES, LANES), LANES)
            for b in range(0, half_words, LANES):
                z = z_v[j * per_half + b // VT, b % VT:b % VT + LANES, cols]
                hit = jnp.where(lab == float(b), 1.0, 0.0)
                d = ((jnp.exp(z - log_norm) - hit) * scale).astype(jnp.bfloat16)
                a_v[b:b + LANES, to_a] = d
                to_dz = pl.ds(pl.multiple_of(j * half_words + b, LANES), LANES)
                dz_v[q % 2, cols, to_dz] = jnp.transpose(d)

    def dz_copy(q, j):
        out_at = (q % 2) * 2 + j
        src = a_v.at[0:half_words, pl.ds(pl.multiple_of(out_at * chunk, chunk), chunk)]
        dst = dz_out.at[pl.ds(pl.multiple_of(j * half_words, half_words), half_words), chunk_at(3 - q)]
        return pltpu.make_async_copy(src, dst, dz_sem.at[out_at])

    def z_reload(s):
        j = s % 2
        src = z_hbm.at[pl.ds((2 - s // 2) * n_vt + j * per_half, per_half)]
        return pltpu.make_async_copy(src, z_v.at[pl.ds(j * per_half, per_half)], z_sem.at[j])

    def first_dz(j, carry):
        dz_pass(jnp.int32(3), j, jnp.int32(0))
        dz_copy(jnp.int32(0), j).start()
        z_reload(j).start()
        return carry

    lax.fori_loop(0, 2, first_dz, 0)

    def prt_copy(s):
        slot = s % 2
        return remote(out_v.at[slot, mine:chunk], prt_v.at[slot], prt_send.at[slot], prt_recv.at[slot], 1)

    d_x = remote(dsend_v.at[0], drecv_v.at[0], d_send.at[0], d_recv.at[0], 2)
    d_y = remote(dsend_v.at[1], drecv_v.at[1], d_send.at[1], d_recv.at[1], 4)

    def stage_copy(s, out, first_out, count):
        j = s % 2
        return pltpu.make_async_copy(
            stage_v.at[j, 0:count],
            out.at[pl.ds(first_out, count), pl.ds(pl.multiple_of(j * NT, NT), NT)],
            stage_sem.at[j],
        )

    def combine(s):
        slot = s % 2
        prt_copy(s).wait_recv()

        @pl.when(s < 2)
        def _():
            dsend_v[slot] = out_v[slot, 0:mine, :] + prt_v[slot]

        @pl.when(s == 0)
        def _():
            d_x.start()

        @pl.when(s == 1)
        def _():
            d_y.start()

        @pl.when(s >= 4)
        def _():
            stage_copy(s, px_out, 0, half).wait()

        @pl.when((s >= 2) & (s < 6) & (slot == 0))
        def _():
            first = pl.multiple_of((2 - s // 2) * half, half)
            stage_v[0, 0:half, :] = out_v[0, 0:half, :] + prt_v[0, 0:half, :]
            hold_v[0, pl.ds(first, half), :] = out_v[0, half:mine, :] + prt_v[0, half:mine, :]
            stage_copy(s, px_out, first, half).start()

        @pl.when((s >= 2) & (s < 6) & (slot == 1))
        def _():
            first = pl.multiple_of((2 - s // 2) * half, half)
            stage_v[1, 0:half, :] = out_v[1, half:mine, :] + prt_v[1, half:mine, :]
            hold_v[1, pl.ds(first, half), :] = out_v[1, 0:half, :] + prt_v[1, 0:half, :]
            stage_copy(s, py_out, first, half).start()

        @pl.when(s >= 6)
        def _():
            stage_v[slot] = out_v[slot, 0:mine, :] + prt_v[slot]
            stage_copy(s, pown_out, 0, mine).start()

        @pl.when(s < 6)
        def _():
            pl.semaphore_signal(credit, inc=1, device_id={"vp": peers[1]}, device_id_type=MESH)

    def backward_step(s, carry):
        q, j = s // 2, s % 2
        slot = s % 2

        @pl.when((s >= 1) & (s < 5))
        def _():
            z_reload(s + 1).start()

        @pl.when(s < 6)
        def _():
            z_reload(s).wait()

        @pl.when(s >= 2)
        def _():
            dz_copy(q - 1, j).wait()
            prt_copy(s).wait_send()

        cols = pl.ds(pl.multiple_of(j * NT, NT), NT)
        out_v[slot] = jnp.dot(dz_v[q % 2], w_v[:, cols], preferred_element_type=jnp.float32)
        dz_pass(jnp.maximum(2 - q, 0), j, q + 1)

        @pl.when(q < 3)
        def _():
            dz_copy(q + 1, j).start()

        @pl.when(s >= 1)
        def _():
            combine(s - 1)

        @pl.when(s >= 2)
        def _():
            pl.semaphore_wait(credit, 1)

        prt_copy(s).start()
        return carry

    lax.fori_loop(0, 8, backward_step, 0)
    combine(jnp.int32(7))

    d_x.wait_recv()
    hold_v[0] += drecv_v[0]
    fin_y = pltpu.make_async_copy(hold_v.at[0], py_out.at[:, 0:NT], fin_sem.at[0])
    fin_y.start()
    d_y.wait_recv()
    hold_v[1] += drecv_v[1]
    fin_x = pltpu.make_async_copy(hold_v.at[1], px_out.at[:, NT:2 * NT], fin_sem.at[1])
    fin_x.start()

    for copy in (*metas, d_x, d_y):
        copy.wait_send()
    for c in range(4):
        for r in range(1, 8):
            st_copy(c, r).wait_send()
    for s in (6, 7):
        prt_copy(s).wait_send()
        stage_copy(s, pown_out, 0, mine).wait()
        dz_copy(3, s % 2).wait()
    fin_y.wait()
    fin_x.wait()


def head(hidden, labels, loss_weight, norm_gain, w_t):
    tok_dev, width = hidden.shape
    tokens = 8 * tok_dev
    vocab_local = w_t.shape[0]
    padded = -(-vocab_local // VT) * VT
    chunk = 2 * tok_dev
    n_vt = padded // VT
    meta = jnp.concatenate(
        [labels.astype(jnp.float32)[None], loss_weight[None], jnp.zeros((6, tok_dev), jnp.float32)], axis=0
    )
    f32, bf16 = jnp.float32, jnp.bfloat16
    hbm = pl.BlockSpec(memory_space=pltpu.MemorySpace.HBM)
    whole = pl.BlockSpec(memory_space=pltpu.VMEM)
    dma = pltpu.SemaphoreType.DMA
    return pl.pallas_call(
        head_kernel,
        out_shape=[
            jax.ShapeDtypeStruct((tokens, width), bf16),
            jax.ShapeDtypeStruct((padded, tokens), bf16),
            jax.ShapeDtypeStruct((tok_dev, width), f32),
            jax.ShapeDtypeStruct((tok_dev, width), f32),
            jax.ShapeDtypeStruct((tok_dev, width), f32),
            jax.ShapeDtypeStruct((3 * n_vt, VT, chunk), f32),
            jax.ShapeDtypeStruct((8, LANES), f32),
        ],
        in_specs=[hbm, whole, whole, hbm],
        out_specs=[hbm] * 6 + [whole],
        scratch_shapes=[
            pltpu.VMEM((padded, width), bf16),
            pltpu.VMEM((tokens, width), bf16),
            pltpu.VMEM((n_vt, VT, chunk), f32),
            pltpu.VMEM((2, chunk, padded), bf16),
            pltpu.VMEM((8, 8, tok_dev), f32),
            pltpu.VMEM((8, tokens), f32),
            pltpu.VMEM((8, chunk), f32),
            pltpu.VMEM((8, chunk), f32),
            pltpu.VMEM((8, chunk), f32),
            pltpu.VMEM((8, 8, tokens), f32),
            pltpu.VMEM((2, chunk, NT), f32),
            pltpu.VMEM((2, tok_dev, NT), f32),
            pltpu.VMEM((2, tok_dev, NT), f32),
            pltpu.VMEM((2, tok_dev, NT), f32),
            pltpu.VMEM((2, tok_dev, NT), f32),
            pltpu.VMEM((2, tok_dev, NT), f32),
            dma((10,)), dma((10,)), dma((7,)), dma((7,)), dma((28,)), dma((28,)),
            dma((2,)), dma((2,)), dma((2,)), dma((2,)),
            dma, dma((n_vt,)), dma((n_vt,)), dma((4,)), dma((4,)), dma((2,)), dma((2,)),
            pltpu.SemaphoreType.REGULAR,
        ],
        compiler_params=pltpu.CompilerParams(
            collective_id=0, has_side_effects=True, vmem_limit_bytes=VMEM_BYTES
        ),
        cost_estimate=pl.CostEstimate(
            flops=4 * tokens * width * padded, bytes_accessed=120_000_000, transcendentals=2 * tokens * padded
        ),
        name="head",
    )(hidden, meta, norm_gain[None], w_t)


def tail_kernel(hidden_ref, gain_ref, own_ref, x_ref, y_ref, dh_ref, dgain_ref, buf, send, recv):
    me = lax.axis_index("vp")
    peers = xor_peers(me)
    barrier = pltpu.get_barrier_semaphore()
    for r in range(1, 8):
        pl.semaphore_signal(barrier, inc=1, device_id={"vp": peers[r]}, device_id_type=MESH)
    rows, width = hidden_ref.shape
    acc = jnp.zeros((8, width), jnp.float32)
    for b in range(0, rows, 32):
        at = slice(b, b + 32)
        x = hidden_ref[at, :].astype(jnp.float32)
        inv_rms = lax.rsqrt(jnp.mean(x * x, axis=-1, keepdims=True) + NORM_EPS)
        n = x * inv_rms
        g = own_ref[at, :] + x_ref[at, :] + y_ref[at, :]
        gn = g * n
        for i in range(0, 32, 8):
            acc += gn[i:i + 8, :]
        u = g * gain_ref[...]
        dh_ref[at, :] = (inv_rms * (u - n * jnp.mean(u * n, axis=-1, keepdims=True))).astype(jnp.bfloat16)
    buf[0] = jnp.sum(acc, axis=0, keepdims=True)
    pl.semaphore_wait(barrier, 7)
    copies = [
        pltpu.make_async_remote_copy(
            src_ref=buf.at[0], dst_ref=buf.at[r], send_sem=send.at[r - 1], recv_sem=recv.at[r - 1],
            device_id={"vp": peers[r]}, device_id_type=MESH,
        )
        for r in range(1, 8)
    ]
    for copy in copies:
        copy.start()
    for copy in copies:
        copy.wait()
    pairs = [buf[2 * r] + buf[2 * r + 1] for r in range(4)]
    dgain_ref[...] = (pairs[0] + pairs[1]) + (pairs[2] + pairs[3])


def tail(hidden, norm_gain, own, from_x, from_y):
    tok_dev, width = hidden.shape
    whole = pl.BlockSpec(memory_space=pltpu.VMEM)
    return pl.pallas_call(
        tail_kernel,
        out_shape=[
            jax.ShapeDtypeStruct((tok_dev, width), jnp.bfloat16),
            jax.ShapeDtypeStruct((1, width), jnp.float32),
        ],
        in_specs=[whole] * 5,
        out_specs=[whole] * 2,
        scratch_shapes=[
            pltpu.VMEM((8, 1, width), jnp.float32),
            pltpu.SemaphoreType.DMA((7,)),
            pltpu.SemaphoreType.DMA((7,)),
        ],
        compiler_params=pltpu.CompilerParams(collective_id=1, has_side_effects=True),
        cost_estimate=pl.CostEstimate(flops=10 * tok_dev * width, bytes_accessed=8_000_000, transcendentals=0),
        name="tail",
    )(hidden, norm_gain[None], own, from_x, from_y)


def weight_grad_kernel(dz_ref, a_ref, out_ref):
    out_ref[...] = jnp.dot(dz_ref[...], a_ref[...], preferred_element_type=jnp.float32)


def weight_grad(dz_t, a_all, vocab_local):
    tokens, width = a_all.shape
    padded = dz_t.shape[0]
    return pl.pallas_call(
        weight_grad_kernel,
        grid=(padded // VT, width // NT),
        out_shape=jax.ShapeDtypeStruct((vocab_local, width), jnp.float32),
        in_specs=[pl.BlockSpec((VT, tokens), lambda i, j: (i, 0)), pl.BlockSpec((tokens, NT), lambda i, j: (0, j))],
        out_specs=pl.BlockSpec((VT, NT), lambda i, j: (i, j)),
        compiler_params=pltpu.CompilerParams(
            vmem_limit_bytes=VMEM_BYTES, dimension_semantics=("arbitrary", "arbitrary")
        ),
        cost_estimate=pl.CostEstimate(
            flops=2 * tokens * width * padded, bytes_accessed=80_000_000, transcendentals=0
        ),
        name="weight_grad",
    )(dz_t, a_all)


def solution(mesh):
    group_size = mesh.shape["vp"]

    def local_step(hidden, labels, loss_weight, norm_gain, w_local):
        vocab_local = w_local.shape[1]
        a_all, dz_t, px, py, pown, _, loss = head(hidden, labels, loss_weight, norm_gain, w_local.T)
        from_x = lax.ppermute(px, "vp", [(i, i ^ 2) for i in range(group_size)])
        from_y = lax.ppermute(py, "vp", [(i, i ^ 4) for i in range(group_size)])
        d_unembed = weight_grad(dz_t, a_all, vocab_local).T
        d_input, d_gain = tail(hidden, norm_gain, pown, from_x, from_y)
        return loss[0, :1], d_input, d_unembed, d_gain[0]

    return jax.shard_map(
        local_step,
        mesh=mesh,
        in_specs=(P(("dp", "vp"), None), P(("dp", "vp")), P(("dp", "vp")), P(None), P(None, "vp")),
        out_specs=(P("dp"), P(("dp", "vp"), None), P("dp", "vp"), P("dp")),
        check_vma=False,
    )
```

time: 379 us -> 189 us (0.50)
  Pallas kernels: 0 us -> 176 us
  matrix products: 129 us -> 0 us
  blocking collectives: 93.3 us -> 0 us
  waiting for transfers between devices: 91.1 us -> 2.95 us
  other arithmetic: 49.8 us -> 2.03 us
  between operations: 14.2 us -> 0.65 us
  local copies, waits for them, and re-layouts: 0.64 us -> 4.86 us
    pallas_call x0 -> x3, Pallas kernels: none -> 176 us  [the longest x1 124 us: head(): pl.pallas_call(head_kernel, out_shape=[jax.ShapeDtypeStruct((tokens, widt...]
    dot_general x3 -> x0, matrix products: 129 us -> none  [the longest x1 43.4 us: local_step(): lax.dot_general(d_logits, w_local, (((1,), (1,)), ((), ())), preferred_el...]
    reduce_scatter x1 -> x0, waiting for transfers between devices: 65.4 us -> none  [local_step(): d_normed = lax.psum_scatter(d_part, 'vp', scatter_dimension=0, tiled=True)]
    psum x2 -> x0, blocking collectives: 46.6 us -> none  [the longest x1 24.2 us: local_step(): sum_exp = lax.psum(jnp.sum(shifted, axis=1), 'vp')]
    convert_element_type x3 -> x1, other arithmetic: 27.6 us -> 0.68 us  [head(): labels.astype(jnp.float32)[None]]
    all_gather x1 -> x0, waiting for transfers between devices: 25.7 us -> none  [local_step(): normed_all = lax.all_gather(normed, 'vp', axis=0, tiled=True)]
    all_gather x2 -> x0, blocking collectives: 24.4 us -> none  [the longest x1 13.7 us: local_step(): weights_all = lax.all_gather(loss_weight, 'vp', axis=0, tiled=True)]
    pmax x1 -> x0, blocking collectives: 22.2 us -> none  [local_step(): row_max = lax.pmax(jnp.max(logits, axis=1), 'vp')]
  transfers between devices with their start and end apart: 2 -> 2, of which waited for: 2 -> 2; matrix products, arithmetic and copies ran while one was open for 12% -> 1% of each run, Pallas kernels for 0% -> 23%
where the time goes in v1:
time: 189 us; the launch traced here: 188 us
  Pallas kernels  176 us (93%)
  local copies, waits for them, and re-layouts  4.86 us (3%)
  waiting for transfers between devices  2.95 us (2%)
  starting transfers between devices  2.16 us (1%)
  other arithmetic  2.03 us (1%)
    pallas_call x1, Pallas kernels, head(): pl.pallas_call(head_kernel, out_shape=[jax.ShapeDtypeStruct((tokens, widt...  124 us
    pallas_call x1, Pallas kernels, weight_grad(): pl.pallas_call(weight_grad_kernel, grid=(padded // VT, width // NT), out_...  42.8 us
    pallas_call x1, Pallas kernels, tail(): pl.pallas_call(tail_kernel, out_shape=[jax.ShapeDtypeStruct((tok_dev, wid...  9.02 us
  transfers between devices with their start and end apart: 2, of which 2 were waited for; matrix products, arithmetic and copies ran while one was open for 1% of the time, Pallas kernels for 23%

profile of v1, /device:TPU:0, one launch (start us, length us, event | category | flops | bytes accessed | tf_op | source)
XLA Modules:
  0.0 188.4 jit_solution(8775161402556121127)
XLA Ops:
  0.6 0.7 convert_element_type.3
  1.3 0.1 pad.2.clone
  1.4 1.3 maximum_maximum_fusion.meta_ref
  2.7 124.0 %head.1 = (bf16[2048,2048]{1,0:T(8,128)(2,1)}, bf16[4096,2048]{1,0:T(8,128)(2,1)}, f32[256,2048]{1,0:T(8,128)}, f32[256,2048]{1,0:T(8,128)}, f32[256,2048]{1,0:T...) custom-call(bf16[256,2048]{1,0:T(8,128)(2,1)} %hidden_ref.1, f32[8,256]{1,0:T(8,128)} %maximum_maximum_fusion.meta_ref, ...), custom_call_target="tpu_custom_call" | custom-call | flops 68719476736 | bytes 120000000 | tf_op jit(solution)/shard_map/head/pallas_call | solution.py:432
  126.8 0.9 collective-permute-start
  127.7 1.2 collective-permute-start.1
  128.9 1.2 slice.3
  130.1 42.8 %weight_grad.1 = f32[4016,2048]{1,0:T(8,128)} custom-call(bf16[4096,2048]{1,0:T(8,128)(2,1)} %get-tuple-element.17.dz_ref, bf16[2048,2048]{1,0:T(8,128)(2,1)} %get-tuple-element.18.a_ref), custom_call_target="tpu_custom_call" | custom-call | flops 34359738368 | bytes 80000000 | tf_op jit(solution)/shard_map/weight_grad/pallas_call | solution.py:542
  172.9 1.9 collective-permute-done.x_ref
  174.7 1.1 collective-permute-done.1.y_ref
  175.8 9.0 %tail.1 = (bf16[256,2048]{1,0:T(8,128)(2,1)}, f32[1,2048]{1,0:T(1,128)}) custom-call(bf16[256,2048]{1,0:T(8,128)(2,1)} %hidden_ref.1, f32[1,2048]{1,0:T(1,128)} %bitcast.9, f32[256,2048]{1,0:T(8,128)} %get-tuple-element.13.own_ref, f32[256,2048]{1,0:T(8,128)} %collective-permute-done.x_ref, f32[256,2048]{1,0:T(8,128)} %collective-permute-done.1.y_ref), custom_call_target="tpu_custom_call" | custom-call | flops 5242880 | bytes 8000000 | tf_op jit(solution)/shard_map/tail/pallas_call | solution.py:516
  184.8 2.3 %copy.11 = bf16[256,2048]{1,0:T(8,128)(2,1)} copy(bf16[256,2048]{1,0:T(8,128)(2,1)} %get-tuple-element.25) | data formatting | bytes 2097152
  187.1 1.3 copy.12
  (1 shorter events, 0.0 us)
Async XLA Ops:
  126.8 47.9 %collective-permute-start = (f32[256,2048]{1,0:T(8,128)}, f32[256,2048]{1,0:T(8,128)}, u32[]{:S(2)}, u32[]{:S(2)}) collective-permute-start(f32[256,2048]{1,0:T(8,128)} %get-tuple-element.14), channel_id=1, source_target_pairs={{0,2},{1,3},{2,0},{3,1},{4,6},{5,7},{6,4},{7,5}} | collective-permute-start | bytes 6291464 | tf_op jit(solution)/shard_map/ppermute | solution.py:564
  127.7 48.1 %collective-permute-start.1 = (f32[256,2048]{1,0:T(8,128)}, f32[256,2048]{1,0:T(8,128)}, u32[]{:S(2)}, u32[]{:S(2)}) collective-permute-start(f32[256,2048]{1,0:T(8,128)} %get-tuple-element.15), channel_id=1, source_target_pairs={{0,4},{1,5},{2,6},{3,7},{4,0},{5,1},{6,2},{7,3}} | collective-permute-start | bytes 6291464 | tf_op jit(solution)/shard_map/ppermute | solution.py:565

commit v2 on v1

v2 whole, which is shorter than its diff:
```python
import functools

import jax
import jax.numpy as jnp
from jax import lax
from jax.experimental import pallas as pl
from jax.experimental.pallas import tpu as pltpu
from jax.sharding import PartitionSpec as P

NORM_EPS = 1e-5
PAD_COLS = 128
LANES = 128
VT = 1024
NT = 1024
EARLY = 512
LOWEST = -3.0e38
MESH = pl.DeviceIdType.MESH
VMEM_BYTES = 67_000_000


def xor_peers(me):
    step_core = 1 - 2 * (me % 2)
    step_x = 2 - 4 * ((me // 2) % 2)
    step_y = 4 - 8 * (me // 4)
    return [me + (r % 2) * step_core + ((r // 2) % 2) * step_x + (r // 4) * step_y for r in range(8)]


def unit_of(rel, half):
    if rel in (0, 1):
        return 2 * rel + half
    if rel in (6, 7):
        return 12 + 2 * (rel - 6) + half
    return {2: 4, 4: 5, 3: 6, 5: 7}[rel] + 4 * half


def head_kernel(
    hidden_hbm, label_ref, weight_ref, gain_ref, w_hbm,
    a_out, dz_out, px_out, py_out, pown_out, z_hbm, loss_ref,
    w_v, a_v, z_e, z_o, dz_e, dz_o, meta_v, row_v, m_v, s_v, t_v, st_v,
    out_v, prt_v, drecv_v, dsend_v, hold_v, first_v, own_v, erecv_v,
    ag_send, ag_recv, meta_send, meta_recv, st_send, st_recv, prt_send, prt_recv, d_send, d_recv, e_send, e_recv,
    in_sem, w_sem, z_sem, a_sem, dz_sem, put_sem, credit,
):
    me = lax.axis_index("vp")
    peers = xor_peers(me)
    vocab_local, width = w_hbm.shape
    vocab_real = 8 * vocab_local - PAD_COLS
    padded = w_v.shape[0]
    n_vt = padded // VT
    tok_dev = hidden_hbm.shape[0]
    chunk = 2 * tok_dev
    half = tok_dev // 2
    quart = tok_dev // 4
    mine = tok_dev
    z_refs = (z_e, z_o)
    dz_refs = (dz_e, dz_o)

    def remote(src, dst, send, recv, rel):
        return pltpu.make_async_remote_copy(
            src_ref=src, dst_ref=dst, send_sem=send, recv_sem=recv,
            device_id={"vp": peers[rel]}, device_id_type=MESH,
        )

    hidden_v = dz_e.at[0:tok_dev, 0:width]
    hidden_copy = pltpu.make_async_copy(hidden_hbm, hidden_v, in_sem)
    hidden_copy.start()
    barrier = pltpu.get_barrier_semaphore()
    for r in range(1, 8):
        pl.semaphore_signal(barrier, inc=1, device_id={"vp": peers[r]}, device_id_type=MESH)

    def w_copy(j):
        hi = min((j + 1) * VT, vocab_local)
        return pltpu.make_async_copy(w_hbm.at[j * VT:hi], w_v.at[j * VT:hi], w_sem.at[j])

    for j in range(n_vt):
        w_copy(j).start()
    meta_v[0, 0:1, :] = label_ref[...].astype(jnp.float32)
    meta_v[0, 1:2, :] = weight_ref[...]

    hidden_copy.wait()
    for b in range(0, tok_dev, 32):
        x = dz_e[b:b + 32, 0:width].astype(jnp.float32)
        inv_rms = lax.rsqrt(jnp.mean(x * x, axis=-1, keepdims=True) + NORM_EPS)
        a_v[b:b + 32, :] = (x * inv_rms * gain_ref[...]).astype(jnp.bfloat16)
    pl.semaphore_wait(barrier, 7)

    def ag(idx, src, dst, count, rel):
        return remote(
            a_v.at[src:src + count], a_v.at[dst:dst + count], ag_send.at[idx], ag_recv.at[idx], rel
        )

    c1, c2, c3 = chunk, 2 * chunk, 3 * chunk
    own_p = ag(0, 0, mine, mine, 1)
    x_h0 = ag(1, 0, c1, half, 2)
    y_h0 = ag(2, 0, c1 + half, half, 4)
    m1_p = ag(3, c1, c1 + mine, mine, 1)
    x_h1 = ag(4, half, c2, half, 2)
    y_h1 = ag(5, half, c2 + half, half, 4)
    m2_p = ag(6, c2, c2 + mine, mine, 1)
    d_x0 = ag(7, c1 + half, c3, quart, 2)
    d_y0 = ag(8, c1 + quart, c3 + quart, quart, 4)
    d_x1 = ag(9, c2 + half, c3 + half, quart, 2)
    d_y1 = ag(10, c2 + quart, c3 + half + quart, quart, 4)
    d_p = ag(11, c3, c3 + mine, mine, 1)
    metas = [remote(meta_v.at[0], meta_v.at[r], meta_send.at[r - 1], meta_recv.at[r - 1], r) for r in range(1, 8)]
    own_p.start()
    for copy in (*metas, x_h0, y_h0, x_h1, y_h1):
        copy.start()
    w_v[vocab_local:padded, :] = jnp.zeros((padded - vocab_local, width), jnp.bfloat16)
    st_v[0] = jnp.zeros(st_v.shape[1:], jnp.float32)

    base_f = (me * vocab_local).astype(jnp.float32)
    valid = jnp.minimum(vocab_local, vocab_real - me * vocab_local)

    def chunk_at(c):
        return pl.ds(pl.multiple_of(c * chunk, chunk), chunk)

    def row_at(row, c, lt):
        return row_v[row:row + 1, pl.ds(pl.multiple_of(c * chunk + lt * LANES, LANES), LANES)]

    def a_copy(c):
        return pltpu.make_async_copy(a_v.at[chunk_at(c)], a_out.at[chunk_at(c)], a_sem.at[c])

    def z_copy(c, j):
        return pltpu.make_async_copy(z_refs[j % 2].at[j // 2], z_hbm.at[c * n_vt + j], z_sem.at[j])

    group = 256
    sub_f = lax.broadcasted_iota(jnp.int32, (8, LANES), 0).astype(jnp.float32)
    step_f = 8.0 * lax.broadcasted_iota(jnp.int32, (group // 8, 8, LANES), 0).astype(jnp.float32)

    def stats_pass(c, j):
        for lt in range(chunk // LANES):
            cols = slice(lt * LANES, (lt + 1) * LANES)
            lab = row_at(0, c, lt) - float(j * VT) - sub_f
            if j == 0:
                m = jnp.full((8, LANES), LOWEST, jnp.float32)
                s = t = jnp.zeros((8, LANES), jnp.float32)
            else:
                m, s, t = m_v[:, cols], s_v[:, cols], t_v[:, cols]
            for b in range(0, VT, group):
                z = z_refs[j % 2][j // 2, b:b + group, cols].reshape(group // 8, 8, LANES)
                m_new = jnp.maximum(m, jnp.max(z, axis=0))
                s = s * jnp.exp(m - m_new) + jnp.sum(jnp.exp(z - m_new[None]), axis=0)
                t += jnp.sum(jnp.where((lab - float(b))[None] == step_f, z, 0.0), axis=0)
                m = m_new
            m_v[:, cols] = m
            s_v[:, cols] = s
            t_v[:, cols] = t

    def st_copy(c, r):
        at = (slice(None), chunk_at(c))
        return remote(st_v.at[(0, *at)], st_v.at[(r, *at)], st_send.at[c * 7 + r - 1], st_recv.at[c * 7 + r - 1], r)

    def send_stats(c):
        m = m_v[...]
        m_row = jnp.max(m, axis=0, keepdims=True)
        st_v[0, 0:1, chunk_at(c)] = m_row
        st_v[0, 1:2, chunk_at(c)] = jnp.sum(s_v[...] * jnp.exp(m - m_row), axis=0, keepdims=True)
        st_v[0, 2:3, chunk_at(c)] = jnp.sum(t_v[...], axis=0, keepdims=True)
        for r in range(1, 8):
            st_copy(c, r).start()

    def logits(c, j, first, count):
        tokens = pl.ds(pl.multiple_of(c * chunk + first, mine), count)
        z_refs[j % 2][j // 2, :, first:first + count] = lax.dot_general(
            w_v[j * VT:(j + 1) * VT, :], a_v[tokens, :], (((1,), (1,)), ((), ())),
            preferred_element_type=jnp.float32,
        )

    def forward_chunk(c, carry):
        @pl.when(c == 0)
        def _():
            w_copy(0).wait()
            w_copy(1).wait()

        @pl.when(c == 1)
        def _():
            x_h0.wait_recv()
            y_h0.wait_recv()
            m1_p.start()
            d_x0.start()
            d_y0.start()

        @pl.when(c == 2)
        def _():
            x_h1.wait_recv()
            y_h1.wait_recv()
            m2_p.start()
            d_x1.start()
            d_y1.start()

        @pl.when(c == 3)
        def _():
            for copy in (d_x0, d_y0, d_x1, d_y1):
                copy.wait_recv()
            d_p.start()

        before = jnp.maximum(c - 1, 0)

        @pl.when(c > 0)
        def _():
            z_copy(before, 0).wait()
            z_copy(before, 1).wait()

        logits(c, 0, 0, mine)
        stats_pass(before, 3)

        @pl.when(c > 0)
        def _():
            send_stats(before)

        logits(c, 1, 0, mine)

        @pl.when(c == 0)
        def _():
            for copy in metas:
                copy.wait_recv()
            for rel in range(8):
                for h in range(2):
                    u = unit_of(rel, h)
                    row_v[:, u * LANES:(u + 1) * LANES] = meta_v[rel, :, h * LANES:(h + 1) * LANES]
            local = row_v[0:1, :] - base_f
            row_v[0:1, :] = jnp.where(local < float(vocab_local), local, -1.0)
            own_p.wait_recv()

        for cc, copy in ((1, m1_p), (2, m2_p), (3, d_p)):
            @pl.when(c == cc)
            def _():
                copy.wait_recv()

        a_copy(c).start()
        logits(c, 0, mine, mine)

        @pl.when(c < 3)
        def _():
            z_copy(c, 0).start()

        logits(c, 1, mine, mine)
        stats_pass(c, 0)

        @pl.when(c < 3)
        def _():
            z_copy(c, 1).start()

        for j in range(2, n_vt):
            @pl.when(c == 0)
            def _():
                w_copy(j).wait()

            @pl.when(c > 0)
            def _():
                z_copy(before, j).wait()

            logits(c, j, 0, chunk)
            stats_pass(c, j - 1)
            if j == n_vt - 1:
                low = (vocab_local - PAD_COLS) // 8 * 8 - j * VT
                ids = j * VT + low + lax.broadcasted_iota(jnp.int32, (VT - low, chunk), 0)
                last = z_refs[j % 2]
                last[j // 2, low:VT, :] = jnp.where(ids < valid, last[j // 2, low:VT, :], -jnp.inf)

            @pl.when(c < 3)
            def _():
                z_copy(c, j).start()

        return carry

    lax.fori_loop(0, 4, forward_chunk, 0)
    stats_pass(3, 3)
    send_stats(3)

    for copy in (x_h0, y_h0, own_p, x_h1, y_h1, m1_p, m2_p, d_x0, d_y0, d_x1, d_y1, d_p):
        copy.wait_send()
    for c in range(4):
        a_copy(c).wait()

    w_row = row_v[1:2, :]
    row_v[3:4, :] = w_row / jnp.sum(w_row)
    for c in range(4):
        for r in range(1, 8):
            st_copy(c, r).wait_recv()
    loss = jnp.zeros((1, LANES), jnp.float32)
    for rel in range(8):
        for h in range(2):
            u = unit_of(rel, h)
            parts = []
            for r in range(8):
                v = unit_of(rel ^ r, h)
                parts.append([st_v[r, i:i + 1, v * LANES:(v + 1) * LANES] for i in range(3)])
            row_max = functools.reduce(jnp.maximum, [p[0] for p in parts])
            row_sum = sum(p[1] * jnp.exp(p[0] - row_max) for p in parts)
            target = sum(p[2] for p in parts)
            log_norm = row_max + jnp.log(row_sum)
            row_v[2:3, u * LANES:(u + 1) * LANES] = log_norm
            loss += row_v[3:4, u * LANES:(u + 1) * LANES] * (log_norm - target)
    loss_ref[...] = jnp.broadcast_to(jnp.sum(loss, axis=1, keepdims=True), loss_ref.shape)

    half_words = 2 * VT
    word_f = lax.broadcasted_iota(jnp.int32, (LANES, LANES), 0).astype(jnp.float32)

    def dz_pass(c, j, parity):
        out_at = parity * 2 + j
        for lt in range(chunk // LANES):
            cols = slice(lt * LANES, (lt + 1) * LANES)
            log_norm, scale = row_at(2, c, lt), row_at(3, c, lt)
            lab = row_at(0, c, lt) - (j * half_words).astype(jnp.float32) - word_f
            to_a = pl.ds(pl.multiple_of(out_at * chunk + lt * LANES, LANES), LANES)
            for b in range(0, half_words, LANES):
                z = z_refs[b // VT][j, b % VT:b % VT + LANES, cols]
                hit = jnp.where(lab == float(b), 1.0, 0.0)
                d = ((jnp.exp(z - log_norm) - hit) * scale).astype(jnp.bfloat16)
                a_v[b:b + LANES, to_a] = d
                to_dz = pl.ds(pl.multiple_of(j * half_words + b, LANES), LANES)
                dz_refs[parity][cols, to_dz] = jnp.transpose(d)

    def dz_copy(c, j, parity):
        out_at = parity * 2 + j
        src = a_v.at[0:half_words, pl.ds(pl.multiple_of(out_at * chunk, chunk), chunk)]
        dst = dz_out.at[pl.ds(pl.multiple_of(j * half_words, half_words), half_words), chunk_at(c)]
        return pltpu.make_async_copy(src, dst, dz_sem.at[out_at])

    def z_reload(c, j):
        return [
            pltpu.make_async_copy(z_hbm.at[c * n_vt + 2 * j + i], z_refs[i].at[j], z_sem.at[2 * j + i])
            for i in range(2)
        ]

    def first_dz(j, carry):
        dz_pass(3, j, 0)
        for copy in z_reload(2, j):
            copy.start()
        return carry

    lax.fori_loop(0, 2, first_dz, 0)

    def prt_copy(slot):
        return remote(out_v.at[slot, mine:chunk], prt_v.at[slot], prt_send.at[slot], prt_recv.at[slot], 1)

    def d_copy(route, j):
        return remote(
            dsend_v.at[j, route * half:(route + 1) * half], drecv_v.at[route, j],
            d_send.at[route * 2 + j], d_recv.at[route * 2 + j], 2 << route,
        )

    def e_copy(route):
        return remote(first_v.at[route, 0, :, 0:EARLY], erecv_v.at[route], e_send.at[route], e_recv.at[route], 2 << route)

    outs = (px_out, py_out)

    def put_first(route, j):
        skip = EARLY if j == 0 else 0
        return pltpu.make_async_copy(
            first_v.at[route, j, :, skip:NT], outs[route].at[:, j * NT + skip - EARLY:(j + 1) * NT - EARLY],
            put_sem.at[route * 2 + j],
        )

    def put_hold(route, j):
        at = width - EARLY + j * NT
        return pltpu.make_async_copy(
            hold_v.at[route, j], outs[route].at[:, at:at + NT], put_sem.at[4 + route * 2 + j]
        )

    def put_own(j):
        return pltpu.make_async_copy(own_v.at[j], pown_out.at[:, j * NT:(j + 1) * NT], put_sem.at[8 + j])

    def combine(s):
        slot = s % 2
        prt_copy(slot).wait_recv()
        for q in range(4):
            for j in range(2):
                @pl.when(s == 2 * q + j)
                def _():
                    if q == 0:
                        dsend_v[j] = out_v[j, 0:mine, :] + prt_v[j]
                        d_copy(0, j).start()
                        d_copy(1, j).start()
                    elif q == 3:
                        own_v[j] = out_v[j, 0:mine, :] + prt_v[j]
                    else:
                        hold_at, first_at = ((0, half), (half, 0))[q - 1]
                        hold_to, first_to = ((0, 1), (1, 0))[q - 1]
                        hold_v[hold_to, j] = out_v[j, hold_at:hold_at + half, :] + prt_v[j, hold_at:hold_at + half, :]
                        first_v[first_to, j] = (
                            out_v[j, first_at:first_at + half, :] + prt_v[j, first_at:first_at + half, :]
                        )
                        if j == 0:
                            e_copy(first_to).start()
                        put_first(first_to, j).start()

        @pl.when(s < 6)
        def _():
            pl.semaphore_signal(credit, inc=1, device_id={"vp": peers[1]}, device_id_type=MESH)

    def backward_step(q, j, parity):
        s = 2 * q + j
        after = jnp.maximum(2 - q, 0)

        @pl.when((q >= 1) & (q < 3))
        def _():
            for copy in z_reload(after, j):
                copy.wait()

        @pl.when(q == 0)
        def _():
            for copy in z_reload(2, j):
                copy.wait()
            dz_copy(3, j, 0).start()

        @pl.when(q >= 1)
        def _():
            dz_copy(4 - q, j, 1 - parity).wait()
            prt_copy(j).wait_send()

        cols = pl.ds(pl.multiple_of(j * NT, NT), NT)
        out_v[j] = jnp.dot(dz_refs[parity][...], w_v[:, cols], preferred_element_type=jnp.float32)
        dz_pass(after, j, 1 - parity)

        @pl.when(q < 2)
        def _():
            for copy in z_reload(1 - q, j):
                copy.start()

        @pl.when(q < 3)
        def _():
            dz_copy(2 - q, j, 1 - parity).start()

        @pl.when(s >= 1)
        def _():
            combine(s - 1)

        @pl.when(s >= 2)
        def _():
            pl.semaphore_wait(credit, 1)

        prt_copy(j).start()

    def backward_pair(qq, carry):
        for parity in range(2):
            def step(j, inner):
                backward_step(2 * qq + parity, j, parity)
                return inner
            lax.fori_loop(0, 2, step, 0)
        return carry

    lax.fori_loop(0, 2, backward_pair, 0)
    combine(jnp.int32(7))

    for j in range(2):
        for route in range(2):
            d_copy(route, j).wait_recv()
            hold_v[1 - route, j] += drecv_v[route, j]
            put_hold(1 - route, j).start()
    put_own(1).start()
    for route in range(2):
        e_copy(route).wait_recv()
        own_v[0, route * half:(route + 1) * half, 0:EARLY] += erecv_v[route]
    put_own(0).start()

    for copy in metas:
        copy.wait_send()
    for c in range(4):
        for r in range(1, 8):
            st_copy(c, r).wait_send()
    for j in range(2):
        prt_copy(j).wait_send()
        dz_copy(0, j, 1).wait()
        put_own(j).wait()
        e_copy(j).wait_send()
        for route in range(2):
            d_copy(route, j).wait_send()
            put_first(route, j).wait()
            put_hold(route, j).wait()


def head(hidden, labels, loss_weight, norm_gain, w_t):
    tok_dev, width = hidden.shape
    tokens = 8 * tok_dev
    vocab_local = w_t.shape[0]
    padded = -(-vocab_local // VT) * VT
    chunk = 2 * tok_dev
    n_vt = padded // VT
    half = tok_dev // 2
    f32, bf16 = jnp.float32, jnp.bfloat16
    hbm = pl.BlockSpec(memory_space=pltpu.MemorySpace.HBM)
    whole = pl.BlockSpec(memory_space=pltpu.VMEM)
    dma = pltpu.SemaphoreType.DMA
    return pl.pallas_call(
        head_kernel,
        out_shape=[
            jax.ShapeDtypeStruct((tokens, width), bf16),
            jax.ShapeDtypeStruct((padded, tokens), bf16),
            jax.ShapeDtypeStruct((half, 2 * width - EARLY), f32),
            jax.ShapeDtypeStruct((half, 2 * width - EARLY), f32),
            jax.ShapeDtypeStruct((tok_dev, width), f32),
            jax.ShapeDtypeStruct((3 * n_vt, VT, chunk), f32),
            jax.ShapeDtypeStruct((8, LANES), f32),
        ],
        in_specs=[hbm, whole, whole, whole, hbm],
        out_specs=[hbm] * 6 + [whole],
        scratch_shapes=[
            pltpu.VMEM((padded, width), bf16),
            pltpu.VMEM((tokens, width), bf16),
            pltpu.VMEM((n_vt // 2, VT, chunk), f32),
            pltpu.VMEM((n_vt // 2, VT, chunk), f32),
            pltpu.VMEM((chunk, padded), bf16),
            pltpu.VMEM((chunk, padded), bf16),
            pltpu.VMEM((8, 8, tok_dev), f32),
            pltpu.VMEM((8, tokens), f32),
            pltpu.VMEM((8, chunk), f32),
            pltpu.VMEM((8, chunk), f32),
            pltpu.VMEM((8, chunk), f32),
            pltpu.VMEM((8, 8, tokens), f32),
            pltpu.VMEM((2, chunk, NT), f32),
            pltpu.VMEM((2, tok_dev, NT), f32),
            pltpu.VMEM((2, 2, half, NT), f32),
            pltpu.VMEM((2, tok_dev, NT), f32),
            pltpu.VMEM((2, 2, half, NT), f32),
            pltpu.VMEM((2, 2, half, NT), f32),
            pltpu.VMEM((2, tok_dev, NT), f32),
            pltpu.VMEM((2, half, EARLY), f32),
            dma((12,)), dma((12,)), dma((7,)), dma((7,)), dma((28,)), dma((28,)),
            dma((2,)), dma((2,)), dma((4,)), dma((4,)), dma((2,)), dma((2,)),
            dma, dma((n_vt,)), dma((n_vt,)), dma((4,)), dma((4,)), dma((10,)),
            pltpu.SemaphoreType.REGULAR,
        ],
        compiler_params=pltpu.CompilerParams(
            collective_id=0, has_side_effects=True, vmem_limit_bytes=VMEM_BYTES
        ),
        cost_estimate=pl.CostEstimate(
            flops=4 * tokens * width * padded, bytes_accessed=120_000_000, transcendentals=2 * tokens * padded
        ),
        name="head",
    )(hidden, labels[None], loss_weight[None], norm_gain[None], w_t)


def tail_kernel(hidden_ref, gain_ref, own_ref, x_ref, y_ref, dh_ref, dgain_ref, buf, send, recv):
    me = lax.axis_index("vp")
    peers = xor_peers(me)
    barrier = pltpu.get_barrier_semaphore()
    for r in range(1, 8):
        pl.semaphore_signal(barrier, inc=1, device_id={"vp": peers[r]}, device_id_type=MESH)
    rows, width = hidden_ref.shape
    half = rows // 2
    early = 2 * width - x_ref.shape[1]
    acc = jnp.zeros((8, width), jnp.float32)
    for b in range(0, rows, 32):
        at = slice(b, b + 32)
        x = hidden_ref[at, :].astype(jnp.float32)
        inv_rms = lax.rsqrt(jnp.mean(x * x, axis=-1, keepdims=True) + NORM_EPS)
        n = x * inv_rms
        part, rest = (x_ref, y_ref) if b < half else (y_ref, x_ref)
        here = slice(b % half, b % half + 32)
        own = own_ref[at, :] + rest[here, width - early:]
        g = jnp.concatenate([own[:, :early], own[:, early:] + part[here, 0:width - early]], axis=1)
        gn = g * n
        for i in range(0, 32, 8):
            acc += gn[i:i + 8, :]
        u = g * gain_ref[...]
        dh_ref[at, :] = (inv_rms * (u - n * jnp.mean(u * n, axis=-1, keepdims=True))).astype(jnp.bfloat16)
    buf[0] = jnp.sum(acc, axis=0, keepdims=True)
    pl.semaphore_wait(barrier, 7)
    copies = [
        pltpu.make_async_remote_copy(
            src_ref=buf.at[0], dst_ref=buf.at[r], send_sem=send.at[r - 1], recv_sem=recv.at[r - 1],
            device_id={"vp": peers[r]}, device_id_type=MESH,
        )
        for r in range(1, 8)
    ]
    for copy in copies:
        copy.start()
    for copy in copies:
        copy.wait()
    pairs = [buf[2 * r] + buf[2 * r + 1] for r in range(4)]
    dgain_ref[...] = (pairs[0] + pairs[1]) + (pairs[2] + pairs[3])


def tail(hidden, norm_gain, own, from_x, from_y):
    tok_dev, width = hidden.shape
    whole = pl.BlockSpec(memory_space=pltpu.VMEM)
    return pl.pallas_call(
        tail_kernel,
        out_shape=[
            jax.ShapeDtypeStruct((tok_dev, width), jnp.bfloat16),
            jax.ShapeDtypeStruct((1, width), jnp.float32),
        ],
        in_specs=[whole] * 5,
        out_specs=[whole] * 2,
        scratch_shapes=[
            pltpu.VMEM((8, 1, width), jnp.float32),
            pltpu.SemaphoreType.DMA((7,)),
            pltpu.SemaphoreType.DMA((7,)),
        ],
        compiler_params=pltpu.CompilerParams(collective_id=1, has_side_effects=True),
        cost_estimate=pl.CostEstimate(flops=10 * tok_dev * width, bytes_accessed=8_000_000, transcendentals=0),
        name="tail",
    )(hidden, norm_gain[None], own, from_x, from_y)


def weight_grad_kernel(dz_ref, a_ref, out_ref):
    out_ref[...] = jnp.dot(dz_ref[...], a_ref[...], preferred_element_type=jnp.float32)


def weight_grad(dz_t, a_all, vocab_local):
    tokens, width = a_all.shape
    padded = dz_t.shape[0]
    return pl.pallas_call(
        weight_grad_kernel,
        grid=(padded // VT, width // NT),
        out_shape=jax.ShapeDtypeStruct((vocab_local, width), jnp.float32),
        in_specs=[pl.BlockSpec((VT, tokens), lambda i, j: (i, 0)), pl.BlockSpec((tokens, NT), lambda i, j: (0, j))],
        out_specs=pl.BlockSpec((VT, NT), lambda i, j: (i, j)),
        compiler_params=pltpu.CompilerParams(
            vmem_limit_bytes=VMEM_BYTES, dimension_semantics=("arbitrary", "arbitrary")
        ),
        cost_estimate=pl.CostEstimate(
            flops=2 * tokens * width * padded, bytes_accessed=80_000_000, transcendentals=0
        ),
        name="weight_grad",
    )(dz_t, a_all)


def solution(mesh):
    group_size = mesh.shape["vp"]

    def local_step(hidden, labels, loss_weight, norm_gain, w_local):
        vocab_local = w_local.shape[1]
        a_all, dz_t, px, py, pown, _, loss = head(hidden, labels, loss_weight, norm_gain, w_local.T)
        from_x = lax.ppermute(px, "vp", [(i, i ^ 2) for i in range(group_size)])
        from_y = lax.ppermute(py, "vp", [(i, i ^ 4) for i in range(group_size)])
        d_unembed = weight_grad(dz_t, a_all, vocab_local).T
        d_input, d_gain = tail(hidden, norm_gain, pown, from_x, from_y)
        return loss[0, :1], d_input, d_unembed, d_gain[0]

    return jax.shard_map(
        local_step,
        mesh=mesh,
        in_specs=(P(("dp", "vp"), None), P(("dp", "vp")), P(("dp", "vp")), P(None), P(None, "vp")),
        out_specs=(P("dp"), P(("dp", "vp"), None), P("dp", "vp"), P("dp")),
        check_vma=False,
    )
```

time: 189 us -> 182 us (0.963)
  waiting for transfers between devices: 2.95 us -> 0.01 us
  other arithmetic: 2.03 us -> 0 us
  transfers between devices with their start and end apart: 2 -> 2, of which waited for: 2 -> 0; matrix products, arithmetic and copies ran while one was open for 1% -> 1% of each run, Pallas kernels for 23% -> 23%
where the time goes in v2:
time: 182 us
  Pallas kernels  176 us (97%)
  local copies, waits for them, and re-layouts  4.77 us (3%)
    pallas_call x1, Pallas kernels, head(): pl.pallas_call(head_kernel, out_shape=[jax.ShapeDtypeStruct((tokens, widt...  123 us
    pallas_call x1, Pallas kernels, weight_grad(): pl.pallas_call(weight_grad_kernel, grid=(padded // VT, width // NT), out_...  42.8 us
    pallas_call x1, Pallas kernels, tail(): pl.pallas_call(tail_kernel, out_shape=[jax.ShapeDtypeStruct((tok_dev, wid...  10.2 us
  transfers between devices with their start and end apart: 2, of which 0 were waited for; matrix products, arithmetic and copies ran while one was open for 1% of the time, Pallas kernels for 23%

profile of v2, /device:TPU:0, one launch (start us, length us, event | category | flops | bytes accessed | tf_op | source)
XLA Modules:
  0.0 182.1 jit_solution(3307972187977950948)
XLA Ops:
  0.6 123.0 %head.1 = (bf16[2048,2048]{1,0:T(8,128)(2,1)}, bf16[4096,2048]{1,0:T(8,128)(2,1)}, f32[128,3584]{1,0:T(8,128)}, f32[128,3584]{1,0:T(8,128)}, f32[256,2048]{1,0:T...) custom-call(bf16[256,2048]{1,0:T(8,128)(2,1)} %hidden_ref.1, s32[1,256]{1,0:T(1,128)} %bitcast.11, ...), custom_call_target="tpu_custom_call" | custom-call | flops 68719476736 | bytes 120000000 | tf_op jit(solution)/shard_map/head/pallas_call | solution.py:487
  123.6 0.6 collective-permute-start
  124.2 0.2 collective-permute-start.1
  124.4 1.2 slice.3
  125.6 42.8 %weight_grad.1 = f32[4016,2048]{1,0:T(8,128)} custom-call(bf16[4096,2048]{1,0:T(8,128)(2,1)} %get-tuple-element.17.dz_ref, bf16[2048,2048]{1,0:T(8,128)(2,1)} %get-tuple-element.18.a_ref), custom_call_target="tpu_custom_call" | custom-call | flops 34359738368 | bytes 80000000 | tf_op jit(solution)/shard_map/weight_grad/pallas_call | solution.py:606
  168.3 0.0 collective-permute-done.x_ref
  168.3 0.0 collective-permute-done.1.y_ref
  168.3 10.2 %tail.1 = (bf16[256,2048]{1,0:T(8,128)(2,1)}, f32[1,2048]{1,0:T(1,128)}) custom-call(bf16[256,2048]{1,0:T(8,128)(2,1)} %hidden_ref.1, f32[1,2048]{1,0:T(1,128)} %bitcast.8, f32[256,2048]{1,0:T(8,128)} %get-tuple-element.13.own_ref, f32[128,3584]{1,0:T(8,128)} %collective-permute-done.x_ref, f32[128,3584]{1,0:T(8,128)} %collective-permute-done.1.y_ref), custom_call_target="tpu_custom_call" | custom-call | flops 5242880 | bytes 8000000 | tf_op jit(solution)/shard_map/tail/pallas_call | solution.py:580
  178.5 2.3 %copy.11 = bf16[256,2048]{1,0:T(8,128)(2,1)} copy(bf16[256,2048]{1,0:T(8,128)(2,1)} %get-tuple-element.25) | data formatting | bytes 2097152
  180.8 1.3 copy.12
Async XLA Ops:
  123.6 44.7 %collective-permute-start = (f32[128,3584]{1,0:T(8,128)}, f32[128,3584]{1,0:T(8,128)}, u32[]{:S(2)}, u32[]{:S(2)}) collective-permute-start(f32[128,3584]{1,0:T(8,128)} %get-tuple-element.14), channel_id=1, source_target_pairs={{0,2},{1,3},{2,0},{3,1},{4,6},{5,7},{6,4},{7,5}} | collective-permute-start | bytes 5505032 | tf_op jit(solution)/shard_map/ppermute | solution.py:628
  124.2 44.1 %collective-permute-start.1 = (f32[128,3584]{1,0:T(8,128)}, f32[128,3584]{1,0:T(8,128)}, u32[]{:S(2)}, u32[]{:S(2)}) collective-permute-start(f32[128,3584]{1,0:T(8,128)} %get-tuple-element.15), channel_id=1, source_target_pairs={{0,4},{1,5},{2,6},{3,7},{4,0},{5,1},{6,2},{7,3}} | collective-permute-start | bytes 5505032 | tf_op jit(solution)/shard_map/ppermute | solution.py:629
